TPU v7x, 32 devices: a whole 2x2x4 slice. The times are simulated.
32 devices in a mesh: seg: 4 (over y, x), lat: 8 (over z, core).
Axes of the slice: x: 2, y: 2, z: 4, core: 2. Of those that a mesh axis runs over, the one named last changes fastest.
Arguments:
- coh_map: bfloat16 [4, 65536, 128], P('seg', 'lat'), may hold values from 0 to 40, as said below
- positions: int32 [4, 1024], P('seg', 'lat'), may hold values from 0 to 16776959, as said below
- counts: int32 [16], P('lat'), may hold values from 1 to 64, as said below
Outputs:
- semi_stat: bfloat16 [1024, 128], P('lat')
- excess: float32 [16, 128], P('lat')
Inputs may be any that keep to these rules, and one draw needn't show every extreme that they name: `coh_map`: nonnegative. `counts`: the first block has 1 valid point and the last block 64. `positions`: the bins are split into 8 aligned slices of 8192 bins; a point's two bins lie in the same slice; in each segment, at most 32 of the 128 points of one index of lat have their bins in one slice, and that most is reached in every draw.
All inputs are finite; a program needn't handle non-finite values.
Results may differ from a plain program's by a relative error of at most 0.001.
Values sent between devices are 32-bit elements; how exact they have to be, the bound alone decides.
A program may use at most 64 MiB of HBM per device.

v0:
```python
import jax
import jax.numpy as jnp
from jax import lax
from jax.sharding import PartitionSpec as P


def routed_sums(positions, coh_map, first_bin):
    seg_count = coh_map.shape[0]
    slice_bins = coh_map.shape[1]
    width = coh_map.shape[2]
    own_rows = positions.shape[1]
    n_lataxis = lax.axis_size("lat")
    slot_limit = 2 * own_rows // n_lataxis
    dest = positions // 256 // slice_bins
    dest_hits = (dest[:, :, None] == lax.broadcasted_iota(jnp.int32, (1, 1, n_lataxis), 2)).astype(
        jnp.int32
    )
    before = jnp.cumsum(dest_hits, axis=1) - dest_hits
    slot = jnp.sum(before * dest_hits, axis=2)
    seg_ids = lax.broadcasted_iota(jnp.int32, positions.shape, 0)
    outgoing = (
        jnp.full((n_lataxis, seg_count, slot_limit), -1, jnp.int32)
        .at[dest, seg_ids, slot]
        .set(positions)
    )
    bin_index = lax.broadcasted_iota(jnp.int32, (1, slice_bins), 1)
    incoming = lax.all_to_all(outgoing, "lat", split_axis=0, concat_axis=0, tiled=True)
    item_count = incoming.shape[2]
    pos_flat = incoming[:, 0, :].reshape(-1)
    live = (pos_flat >= 0)[:, None]
    rel_bin = (pos_flat // 256 - first_bin)[:, None]
    fraction = (pos_flat % 256).astype(jnp.float32)[:, None] / 256.0
    weights = jnp.where(live & (bin_index == rel_bin), 1.0 - fraction, 0.0) + jnp.where(
        live & (bin_index == rel_bin + 1), fraction, 0.0
    )
    rows = jnp.dot(weights.astype(jnp.bfloat16), coh_map[0], preferred_element_type=jnp.float32)
    row_list = [rows.reshape(n_lataxis, item_count, width)]
    stacked = jnp.stack(row_list, axis=1)
    returned = lax.all_to_all(stacked, "lat", split_axis=0, concat_axis=0, tiled=True)
    by_segment = returned.transpose(1, 0, 2, 3).reshape(seg_count, n_lataxis * slot_limit, width)
    flat_index = dest * slot_limit + slot
    picked = jnp.take_along_axis(by_segment, flat_index[:, :, None], axis=1)
    return jnp.sum(picked, axis=0)


def shards(coh_map, positions, counts):
    seg_count = coh_map.shape[0]
    slice_bins = coh_map.shape[1]
    first_bin = lax.axis_index("lat") * slice_bins
    n_segaxis = lax.axis_size("seg")
    total_segs = seg_count * n_segaxis
    own_rows = positions.shape[1]
    local_sums_rows = routed_sums(positions, coh_map, first_bin)
    summed = lax.psum(local_sums_rows, "seg")
    semi_stat = summed / total_segs
    block_count = counts.shape[0]
    block_size = own_rows // block_count
    grouped = semi_stat.reshape(block_count, block_size, semi_stat.shape[1])
    slot_index = lax.broadcasted_iota(jnp.int32, (block_count, block_size, 1), 1)
    live_mask = slot_index < counts[:, None, None]
    block_sums = jnp.sum(jnp.where(live_mask, grouped, 0.0), axis=1)
    count_float = counts.astype(jnp.float32)
    block_means = block_sums / count_float[:, None]
    column_sums, total_count = lax.psum((jnp.sum(block_sums, axis=0), jnp.sum(count_float)), "lat")
    global_mean = column_sums / total_count
    excess = block_means - global_mean[None, :]
    return (semi_stat.astype(jnp.bfloat16), excess)


def solution(mesh):
    in_specs = (P("seg", "lat", None), P("seg", "lat"), P("lat"))
    out_specs = (P("lat", None), P("lat", None))
    return jax.shard_map(shards, mesh=mesh, in_specs=in_specs, out_specs=out_specs, check_vma=False)
```

profile of v0, /device:TPU:0, one launch (start us, length us, event | category | flops | bytes accessed | tf_op | source)
XLA Modules:
  0.0 125.4 jit_solution(7126655053401794815)
XLA Ops:
  7.2 0.0 copy-start
  7.2 0.8 fusion.19
  8.0 0.1 fusion.12
  8.1 0.2 reduce_window_sum.11
  8.3 0.2 select_reduce_fusion.2
  8.5 0.6 broadcast.427
  9.1 19.9 %scatter_fusion = s32[8,32]{1,0:T(8,128)} fusion(s32[8,32]{1,0:T(8,128)} %broadcast.427, s32[128]{0:T(128)S(1)} %fusion.21, s32[128]{0:T(128)} %bitcast.50), kind=kCustom, calls=%fused_computation.1 | custom fusion | bytes 2560 | tf_op jit(solution)/shard_map/scatter | solution.py:24
  29.0 6.4 %all-to-all-start = ((s32[8,1,32]{2,1,0:T(1,128)}), s32[8,1,32]{2,1,0:T(1,128)S(1)}, u32[]{:S(2)}, u32[]{:S(2)}) async-start(s32[8,1,32]{2,1,0:T(1,128)} %bitcast.9), calls=%async_computation | async-start | bytes 8192 | tf_op jit(solution)/shard_map/all_to_all | solution.py:27
  35.3 0.7 iota_compare_fusion.3
  36.0 4.8 %all-to-all-done = s32[8,1,32]{2,1,0:T(1,128)S(1)} async-done(((s32[8,1,32]{2,1,0:T(1,128)}), s32[8,1,32]{2,1,0:T(1,128)S(1)}, u32[]{:S(2)}, u32[]{:S(2)}) %all-to-all-start) | async-done | bytes 1056 | tf_op jit(solution)/shard_map/all_to_all | solution.py:27
  40.9 0.0 copy-done
  40.9 0.0 copy-start.1
  40.9 5.0 %fusion.7 = f32[8,1,32,128]{3,2,1,0:T(8,128)} fusion(bf16[1,8192,128]{2,1,0:T(8,128)(2,1)S(1)} %copy-done, f32[8,32]{1,0:T(8,128)S(1)} %get-tuple-element.5, s32[8,32]{1,0:T(8,128)S(1)} %get-tuple-element.6, f32[8,32]{1,0:T(8,128)S(1)} %get-tuple-element.4, s32[8,32]{1,0:T(8,128)S(1)} %get-tuple-element.7, pred[8,32]{1,0:T(8,128)(4,1)S(1)} %broadcast_compare_fusion), kind=kOutput, calls=%fused_computation.11 | convolution fusion | flops 553648128 | bytes 2232576 | tf_op jit(solution)/shard_map/dot_general | solution.py:36
  45.9 3.4 %all-to-all-start.1 = ((f32[8,1,32,128]{3,2,1,0:T(8,128)}), f32[8,1,32,128]{3,2,1,0:T(8,128)S(1)}, u32[]{:S(2)}, u32[]{:S(2)}) async-start(f32[8,1,32,128]{3,2,1,0:T(8,128)} %fusion.7), calls=%async_computation.1 | async-start | bytes 262144 | tf_op jit(solution)/shard_map/all_to_all | solution.py:39
  49.2 0.0 all-reduce.3.cloned.1.call-start
  49.3 0.0 copy-done.1
  49.3 0.1 lt.77
  49.4 6.5 %all-to-all-done.1 = f32[8,1,32,128]{3,2,1,0:T(8,128)S(1)} async-done(((f32[8,1,32,128]{3,2,1,0:T(8,128)}), f32[8,1,32,128]{3,2,1,0:T(8,128)S(1)}, u32[]{:S(2)}, u32[]{:S(2)}) %all-to-all-start.1) | async-done | bytes 131104 | tf_op jit(solution)/shard_map/all_to_all | solution.py:39
  55.9 0.6 gather_fusion
  56.6 0.7 broadcast_select_fusion
  57.3 0.0 all-reduce.3.cloned.1.call-update
  57.3 0.6 convert_reduce_fusion
  57.9 40.4 %all-reduce.3.cloned.1.call-done = f32[128,128]{1,0:T(8,128)} async-done(((f32[128,128]{1,0:T(8,128)}), f32[128,128]{1,0:T(8,128)}) %all-reduce.3.cloned.1.call-update) | async-done | bytes 65552 | tf_op jit(solution)/shard_map/psum | solution.py:54
  98.3 1.5 %select_reduce_fusion = (f32[128]{0:T(128)S(1)}, bf16[128,128]{1,0:T(8,128)(2,1)}) fusion(pred[128]{0:T(512)(128)(4,1)S(1)} %lt.77, f32[128,128]{1,0:T(8,128)} %all-reduce.3.cloned.1.call-done), kind=kLoop, calls=%fused_computation.12 | loop fusion | flops 65408 | bytes 98944 | tf_op jit(solution)/shard_map/reduce_sum | solution.py:64
  99.8 16.6 %all-reduce = (f32[128]{0:T(128)S(1)}, f32[]{:T(128)}) all-reduce(f32[128]{0:T(128)S(1)} %get-tuple-element.10, f32[]{:T(128)} %convert_reduce_fusion), channel_id=1, replica_groups=mesh['seg'=4,'lat'=8] {'lat'}, use_global_device_ids=true, to_apply=%region_6.7 | all-reduce | flops 129 | bytes 1032 | tf_op jit(solution)/shard_map/psum | solution.py:64
  116.3 0.6 broadcast_divide_fusion
  117.0 0.9 select_reduce_fusion.1
  117.9 0.6 divide_subtract_fusion
  (11 shorter events, 0.1 us)
Async XLA Ops:
  7.2 33.7 %copy-start = (bf16[1,8192,128]{2,1,0:T(8,128)(2,1)S(1)}, bf16[1,8192,128]{2,1,0:T(8,128)(2,1)}, u32[]{:S(2)}) copy-start(bf16[1,8192,128]{2,1,0:T(8,128)(2,1)} %param.3) | copy-start | bytes 6291460
  29.0 11.9 %all-to-all-start = ((s32[8,1,32]{2,1,0:T(1,128)}), s32[8,1,32]{2,1,0:T(1,128)S(1)}, u32[]{:S(2)}, u32[]{:S(2)}) async-start(s32[8,1,32]{2,1,0:T(1,128)} %bitcast.9), calls=%async_computation | async-start | bytes 8192 | tf_op jit(solution)/shard_map/all_to_all | solution.py:27
  40.9 8.4 %copy-start.1 = (s32[2]{0:T(128)S(1)}, s32[2]{0:T(128)}, u32[]{:S(2)}) copy-start(s32[2]{0:T(128)} %param.5) | copy-start | bytes 28
  45.9 10.1 %all-to-all-start.1 = ((f32[8,1,32,128]{3,2,1,0:T(8,128)}), f32[8,1,32,128]{3,2,1,0:T(8,128)S(1)}, u32[]{:S(2)}, u32[]{:S(2)}) async-start(f32[8,1,32,128]{3,2,1,0:T(8,128)} %fusion.7), calls=%async_computation.1 | async-start | bytes 262144 | tf_op jit(solution)/shard_map/all_to_all | solution.py:39
  49.2 49.1 %all-reduce.3.cloned.1.call-start = ((), (), s32[]{:S(2)}) async-start(), calls=%async_computation.2 | async-start | bytes 131072 | tf_op jit(solution)/shard_map/psum | solution.py:54
Sparse Core Ops, SparseCore 0:
  57.4 40.8 all-reduce.2
where the time goes:
time: 126 us; the launch traced here: 125 us
  waiting for transfers between devices  51.7 us (41%)
  local copies, waits for them, and re-layouts  21.2 us (17%)
  blocking collectives  16.6 us (13%)
  between operations  14.1 us (11%)
  starting transfers between devices  9.76 us (8%)
  other arithmetic  7.05 us (6%)
  matrix products  4.96 us (4%)
    psum x1, waiting for transfers between devices, shards(): summed = lax.psum(local_sums_rows, 'seg')  40.4 us
    scatter x1, local copies, waits for them, and re-layouts, routed_sums(): outgoing = jnp.full((n_lataxis, seg_count, slot_limit), -1, jnp.int32).at...  19.9 us
    psum x1, blocking collectives, shards(): lax.psum((jnp.sum(block_sums, axis=0), jnp.sum(count_float)), 'lat')  16.6 us
    all_to_all x1, waiting for transfers between devices, routed_sums(): lax.all_to_all(stacked, 'lat', split_axis=0, concat_axis=0, tiled=True)  6.51 us
    all_to_all x1, starting transfers between devices, routed_sums(): lax.all_to_all(outgoing, 'lat', split_axis=0, concat_axis=0, tiled=True)  6.35 us
    dot_general x1, matrix products, routed_sums(): jnp.dot(weights.astype(jnp.bfloat16), coh_map[0], preferred_element_type=...  4.96 us
    all_to_all x1, waiting for transfers between devices, routed_sums(): lax.all_to_all(outgoing, 'lat', split_axis=0, concat_axis=0, tiled=True)  4.77 us
    all_to_all x1, starting transfers between devices, routed_sums(): lax.all_to_all(stacked, 'lat', split_axis=0, concat_axis=0, tiled=True)  3.37 us
  transfers between devices with their start and end apart: 3, of which 3 were waited for; matrix products, arithmetic and copies ran while one was open for 1% of the time, Pallas kernels for 0%

commit v1 on v0

--- a/solution.py
+++ b/solution.py
@@ -2,6 +2,14 @@
 import jax.numpy as jnp
 from jax import lax
 from jax.sharding import PartitionSpec as P
+
+
+def add_in_pairs(shard, mesh_axis):
+    size, total = (lax.axis_size(mesh_axis), shard)
+    for far in [1 << k for k in range(size.bit_length() - 1)]:
+        swap = [(i, i ^ far) for i in range(size)]
+        total = total + lax.ppermute(total, mesh_axis, swap)
+    return total
 
 
 def routed_sums(positions, coh_map, first_bin):
@@ -51,7 +59,7 @@
     total_segs = seg_count * n_segaxis
     own_rows = positions.shape[1]
     local_sums_rows = routed_sums(positions, coh_map, first_bin)
-    summed = lax.psum(local_sums_rows, "seg")
+    summed = add_in_pairs(local_sums_rows, "seg")
     semi_stat = summed / total_segs
     block_count = counts.shape[0]
     block_size = own_rows // block_count

time: 126 us -> 75.9 us (0.60)
  waiting for transfers between devices: 51.7 us -> 16.9 us
  between operations: 14.1 us -> 0.77 us
  starting transfers between devices: 9.76 us -> 12.9 us
  other arithmetic: 7.05 us -> 4.19 us
  blocking collectives: 16.6 us -> 14.2 us
    psum x1 -> x0, waiting for transfers between devices: 40.4 us -> none  [shards(): summed = lax.psum(local_sums_rows, 'seg')]
    ppermute x0 -> x2, waiting for transfers between devices: none -> 4.76 us  [add_in_pairs(): total = total + lax.ppermute(total, mesh_axis, swap)]
    ppermute x0 -> x2, starting transfers between devices: none -> 3.14 us  [add_in_pairs(): total = total + lax.ppermute(total, mesh_axis, swap)]
    psum x1, blocking collectives: 16.6 us -> 14.2 us  [shards(): lax.psum((jnp.sum(block_sums, axis=0), jnp.sum(count_float)), 'lat')]
  transfers between devices with their start and end apart: 3 -> 4, of which waited for: 3 -> 4; matrix products, arithmetic and copies ran while one was open for 1% -> 1% of each run, Pallas kernels for 0% -> 0%
where the time goes in v1:
time: 75.9 us; the launch traced here: 75.1 us
  local copies, waits for them, and re-layouts  21.2 us (28%)
  waiting for transfers between devices  16.9 us (22%)
  blocking collectives  14.2 us (19%)
  starting transfers between devices  12.9 us (17%)
  matrix products  4.96 us (7%)
  other arithmetic  4.19 us (6%)
  between operations  0.77 us (1%)
    scatter x1, local copies, waits for them, and re-layouts, routed_sums(): outgoing = jnp.full((n_lataxis, seg_count, slot_limit), -1, jnp.int32).at...  19.9 us
    psum x1, blocking collectives, shards(): lax.psum((jnp.sum(block_sums, axis=0), jnp.sum(count_float)), 'lat')  14.2 us
    all_to_all x1, waiting for transfers between devices, routed_sums(): lax.all_to_all(stacked, 'lat', split_axis=0, concat_axis=0, tiled=True)  6.66 us
    all_to_all x1, starting transfers between devices, routed_sums(): lax.all_to_all(outgoing, 'lat', split_axis=0, concat_axis=0, tiled=True)  6.35 us
    all_to_all x1, waiting for transfers between devices, routed_sums(): lax.all_to_all(outgoing, 'lat', split_axis=0, concat_axis=0, tiled=True)  5.5 us
    dot_general x1, matrix products, routed_sums(): jnp.dot(weights.astype(jnp.bfloat16), coh_map[0], preferred_element_type=...  4.96 us
    ppermute x2, waiting for transfers between devices, add_in_pairs(): total = total + lax.ppermute(total, mesh_axis, swap)  4.76 us
    all_to_all x1, starting transfers between devices, routed_sums(): lax.all_to_all(stacked, 'lat', split_axis=0, concat_axis=0, tiled=True)  3.37 us
  transfers between devices with their start and end apart: 4, of which 4 were waited for; matrix products, arithmetic and copies ran while one was open for 1% of the time, Pallas kernels for 0%

profile of v1, /device:TPU:0, one launch (start us, length us, event | category | flops | bytes accessed | tf_op | source)
XLA Modules:
  0.0 75.1 jit_solution(16792370357827158864)
XLA Ops:
  0.6 0.0 copy-start
  0.6 0.8 %fusion.19 = (s32[1,128,1]{1,2,0:T(1,128)S(1)}, s32[1,128]{1,0:T(1,128)S(1)}) fusion(s32[1,128]{1,0:T(1,128)} %param.4), kind=kLoop, calls=%fused_computation.56 | loop fusion | flops 4224 | bytes 1536 | tf_op jit(solution)/shard_map/broadcast_in_dim | solution.py:32
  1.5 0.1 fusion.12
  1.6 0.2 reduce_window_sum.11
  1.7 0.2 select_reduce_fusion.2
  2.0 0.6 broadcast.427
  2.6 19.9 %scatter_fusion = s32[8,32]{1,0:T(8,128)} fusion(s32[8,32]{1,0:T(8,128)} %broadcast.427, s32[128]{0:T(128)S(1)} %fusion.21, s32[128]{0:T(128)} %bitcast.50), kind=kCustom, calls=%fused_computation.1 | custom fusion | bytes 2560 | tf_op jit(solution)/shard_map/scatter | solution.py:32
  22.4 6.4 %all-to-all-start = ((s32[8,1,32]{2,1,0:T(1,128)}), s32[8,1,32]{2,1,0:T(1,128)S(1)}, u32[]{:S(2)}, u32[]{:S(2)}) async-start(s32[8,1,32]{2,1,0:T(1,128)} %bitcast.9), calls=%async_computation | async-start | bytes 8192 | tf_op jit(solution)/shard_map/all_to_all | solution.py:35
  28.8 5.5 %all-to-all-done = s32[8,1,32]{2,1,0:T(1,128)S(1)} async-done(((s32[8,1,32]{2,1,0:T(1,128)}), s32[8,1,32]{2,1,0:T(1,128)S(1)}, u32[]{:S(2)}, u32[]{:S(2)}) %all-to-all-start) | async-done | bytes 1056 | tf_op jit(solution)/shard_map/all_to_all | solution.py:35
  34.3 0.0 copy-done
  34.3 0.0 copy-start.1
  34.4 5.0 %fusion.7 = f32[8,1,32,128]{3,2,1,0:T(8,128)} fusion(bf16[1,8192,128]{2,1,0:T(8,128)(2,1)S(1)} %copy-done, f32[8,32]{1,0:T(8,128)S(1)} %get-tuple-element.5, s32[8,32]{1,0:T(8,128)S(1)} %get-tuple-element.6, f32[8,32]{1,0:T(8,128)S(1)} %get-tuple-element.4, s32[8,32]{1,0:T(8,128)S(1)} %get-tuple-element.7, pred[8,32]{1,0:T(8,128)(4,1)S(1)} %broadcast_compare_fusion), kind=kOutput, calls=%fused_computation.11 | convolution fusion | flops 553648128 | bytes 2232576 | tf_op jit(solution)/shard_map/dot_general | solution.py:44
  39.3 3.4 %all-to-all-start.1 = ((f32[8,1,32,128]{3,2,1,0:T(8,128)}), f32[8,1,32,128]{3,2,1,0:T(8,128)S(1)}, u32[]{:S(2)}, u32[]{:S(2)}) async-start(f32[8,1,32,128]{3,2,1,0:T(8,128)} %fusion.7), calls=%async_computation.1 | async-start | bytes 262144 | tf_op jit(solution)/shard_map/all_to_all | solution.py:47
  42.7 6.7 %all-to-all-done.1 = f32[8,1,32,128]{3,2,1,0:T(8,128)S(1)} async-done(((f32[8,1,32,128]{3,2,1,0:T(8,128)}), f32[8,1,32,128]{3,2,1,0:T(8,128)S(1)}, u32[]{:S(2)}, u32[]{:S(2)}) %all-to-all-start.1) | async-done | bytes 131104 | tf_op jit(solution)/shard_map/all_to_all | solution.py:47
  49.4 0.6 gather_fusion
  50.0 0.1 broadcast_select_fusion
  50.1 1.6 %collective-permute-start = (f32[128,128]{1,0:T(8,128)S(1)}, f32[128,128]{1,0:T(8,128)S(1)}, u32[]{:S(2)}, u32[]{:S(2)}) collective-permute-start(f32[128,128]{1,0:T(8,128)S(1)} %broadcast_select_fusion), channel_id=1, source_target_pairs={{0,8},{8,0},{16,24},{24,16},{1,9},{9,1},{17,25},{25,17},{2,10},{10... | collective-permute-start | bytes 196616 | tf_op jit(solution)/shard_map/ppermute | solution.py:11
  51.7 0.0 copy-done.1
  51.7 0.1 iota_compare_fusion.3
  51.8 0.1 lt.77
  51.8 2.6 %collective-permute-done = f32[128,128]{1,0:T(8,128)S(1)} collective-permute-done((f32[128,128]{1,0:T(8,128)S(1)}, f32[128,128]{1,0:T(8,128)S(1)}, u32[]{:S(2)}, u32[]{:S(2)}) %collective-permute-start) | collective-permute-done | bytes 65568 | tf_op jit(solution)/shard_map/ppermute | solution.py:11
  54.4 0.1 fusion.26
  54.5 1.6 %collective-permute-start.1 = (f32[128,128]{1,0:T(8,128)S(1)}, f32[128,128]{1,0:T(8,128)S(1)}, u32[]{:S(2)}, u32[]{:S(2)}) collective-permute-start(f32[128,128]{1,0:T(8,128)S(1)} %fusion.26), channel_id=1, source_target_pairs={{0,16},{8,24},{16,0},{24,8},{1,17},{9,25},{17,1},{25,9},{2,18},{10... | collective-permute-start | bytes 196616 | tf_op jit(solution)/shard_map/ppermute | solution.py:11
  56.1 0.6 convert_reduce_fusion
  56.7 2.1 %collective-permute-done.1 = f32[128,128]{1,0:T(8,128)S(1)} collective-permute-done((f32[128,128]{1,0:T(8,128)S(1)}, f32[128,128]{1,0:T(8,128)S(1)}, u32[]{:S(2)}, u32[]{:S(2)}) %collective-permute-start.1) | collective-permute-done | bytes 65568 | tf_op jit(solution)/shard_map/ppermute | solution.py:11
  58.9 0.6 select_reduce_fusion
  59.5 14.2 %all-reduce = (f32[128]{0:T(128)S(1)}, f32[]{:T(128)}) all-reduce(f32[128]{0:T(128)S(1)} %get-tuple-element.10, f32[]{:T(128)} %convert_reduce_fusion), channel_id=1, replica_groups=mesh['seg'=4,'lat'=8] {'lat'}, use_global_device_ids=true, to_apply=%region_5.6 | all-reduce | flops 129 | bytes 1032 | tf_op jit(solution)/shard_map/psum | solution.py:72
  73.7 0.6 broadcast_divide_fusion
  74.4 0.1 select_reduce_fusion.1
  74.5 0.6 divide_subtract_fusion
  (11 shorter events, 0.1 us)
Async XLA Ops:
  0.6 33.7 %copy-start = (bf16[1,8192,128]{2,1,0:T(8,128)(2,1)S(1)}, bf16[1,8192,128]{2,1,0:T(8,128)(2,1)}, u32[]{:S(2)}) copy-start(bf16[1,8192,128]{2,1,0:T(8,128)(2,1)} %param.3) | copy-start | bytes 6291460
  22.4 11.9 %all-to-all-start = ((s32[8,1,32]{2,1,0:T(1,128)}), s32[8,1,32]{2,1,0:T(1,128)S(1)}, u32[]{:S(2)}, u32[]{:S(2)}) async-start(s32[8,1,32]{2,1,0:T(1,128)} %bitcast.9), calls=%async_computation | async-start | bytes 8192 | tf_op jit(solution)/shard_map/all_to_all | solution.py:35
  34.3 17.3 %copy-start.1 = (s32[2]{0:T(128)S(1)}, s32[2]{0:T(128)}, u32[]{:S(2)}) copy-start(s32[2]{0:T(128)} %param.5) | copy-start | bytes 28
  39.3 10.1 %all-to-all-start.1 = ((f32[8,1,32,128]{3,2,1,0:T(8,128)}), f32[8,1,32,128]{3,2,1,0:T(8,128)S(1)}, u32[]{:S(2)}, u32[]{:S(2)}) async-start(f32[8,1,32,128]{3,2,1,0:T(8,128)} %fusion.7), calls=%async_computation.1 | async-start | bytes 262144 | tf_op jit(solution)/shard_map/all_to_all | solution.py:47
  50.1 4.3 %collective-permute-start = (f32[128,128]{1,0:T(8,128)S(1)}, f32[128,128]{1,0:T(8,128)S(1)}, u32[]{:S(2)}, u32[]{:S(2)}) collective-permute-start(f32[128,128]{1,0:T(8,128)S(1)} %broadcast_select_fusion), channel_id=1, source_target_pairs={{0,8},{8,0},{16,24},{24,16},{1,9},{9,1},{17,25},{25,17},{2,10},{10... | collective-permute-start | bytes 196616 | tf_op jit(solution)/shard_map/ppermute | solution.py:11
  54.5 4.3 %collective-permute-start.1 = (f32[128,128]{1,0:T(8,128)S(1)}, f32[128,128]{1,0:T(8,128)S(1)}, u32[]{:S(2)}, u32[]{:S(2)}) collective-permute-start(f32[128,128]{1,0:T(8,128)S(1)} %fusion.26), channel_id=1, source_target_pairs={{0,16},{8,24},{16,0},{24,8},{1,17},{9,25},{17,1},{25,9},{2,18},{10... | collective-permute-start | bytes 196616 | tf_op jit(solution)/shard_map/ppermute | solution.py:11
